TPU v7x, 32 devices: a whole 2x2x4 slice. The times are simulated.
32 devices in a mesh: row: 8 (over z, y), col: 4 (over x, core).
Axes of the slice: x: 2, y: 2, z: 4, core: 2. Of those that a mesh axis runs over, the one named last changes fastest.
Arguments:
- tracer: float32 [128, 128, 512], P(None, 'row', 'col'), may hold values from -6 to 6
- symbol_x: float32 [128], replicated, may hold values from 0.3 to 3
- symbol_y: float32 [128], replicated, may hold values from 0.3 to 3
- symbol_z: float32 [512], replicated, may hold values from 0.3 to 3
Outputs:
- spectrum: float32 [128, 128, 512], P('row', 'col')
All inputs are finite; a program needn't handle non-finite values.
Results may differ from a plain program's by a relative error of at most 0.000075.
Values sent between devices are 32-bit elements; how exact they have to be, the bound alone decides.
A program may use at most 64 MiB of HBM per device.

v0:
```python
import functools

import jax
import jax.numpy as jnp
import ml_dtypes
import numpy as np
from jax import lax
from jax.experimental import pallas as pl
from jax.experimental.pallas import tpu as pltpu
from jax.sharding import PartitionSpec as P

MESH = pl.DeviceIdType.MESH
F32 = jnp.float32
BF16 = jnp.bfloat16
PIECES = 4
LAG = 1


def table_halves(count):
    rank = np.arange(1, count + 1)
    turns = np.outer(rank, rank) % (2 * count + 2)
    table = np.sin(np.pi / (count + 1) * turns) * np.sqrt(2.0 / (count + 1))
    high = table.astype(ml_dtypes.bfloat16)
    low = (table - high.astype(np.float64)).astype(ml_dtypes.bfloat16)
    return high, low


def halves(values):
    high = values.astype(BF16)
    return high, (values - high.astype(F32)).astype(BF16)


def dot(a, b):
    return jnp.dot(a, b, preferred_element_type=F32)


def from_left(stacked, values):
    rows = stacked.shape[0] // 2
    high, low = halves(values)
    both = dot(stacked, high)
    return both[:rows] + both[rows:] + dot(stacked[:rows], low)


def kernel(
    n, m, pieces, groups, block,
    field, tab_x, tab_y, tab_zh, tab_zl, sx, sy, sz, out,
    d, s, r, y, c, f, tx, ty, tzh, tzl, colx, coly, vx, vy, vz,
    in_sem, tab_sem, send_r, recv_r, send_c, recv_c,
):
    lag = min(LAG, pieces)
    me_r, me_c = lax.axis_index("row"), lax.axis_index("col")
    depth, ys, zs = d.shape
    each = r.shape[0] // pieces
    per = n * each
    yc = y.shape[3]
    loads = [(field, d, 0), (tab_x, tx, 1), (tab_y, ty, 2), (tab_zh, tzh, 3), (tab_zl, tzl, 4)]
    loads += [(sx, vx, 5), (sy, vy, 6), (sz, vz, 7)]
    loads = [pltpu.make_async_copy(a, b, in_sem.at[i]) for a, b, i in loads]
    for load in loads:
        load.start()

    barrier = pltpu.get_barrier_semaphore()

    def greet(axis, me, size):
        def one(i, _):
            pl.semaphore_signal(
                barrier, inc=1, device_id={axis: lax.rem(me + i, size)}, device_id_type=MESH
            )
            return 0

        lax.fori_loop(1, size, one, 0)

    greet("row", me_r, n)
    greet("col", me_c, m)

    loads[0].wait()
    loads[1].wait()
    lanes = d.reshape(depth * ys, zs)
    modes = s.reshape(s.shape[0] * ys, zs)

    def transform_x(first, count):
        rows = count * per
        stacked = tx[2 * first * per : 2 * (first + count) * per]

        def pair(i, _):
            got = jnp.concatenate(
                [lanes[pl.ds(2 * i + h, depth, stride=ys), :] for h in range(2)], axis=1
            )
            got = from_left(stacked, got)
            for h in range(2):
                modes[pl.ds(first * per * ys + 2 * i + h, rows, stride=ys), :] = got[
                    :, h * zs : (h + 1) * zs
                ]
            return 0

        lax.fori_loop(0, ys // 2, pair, 0, unroll=True)

    def send_rows(k):
        def one(i, _):
            to = lax.rem(me_r + 1 + i, n)
            pltpu.make_async_remote_copy(
                src_ref=s.at[pl.ds(k * per + to * each, each)],
                dst_ref=r.at[pl.ds(k * each, each), pl.ds(pl.multiple_of(me_r * ys, ys), ys), :],
                send_sem=send_r.at[k],
                recv_sem=recv_r.at[k],
                device_id={"row": to},
                device_id_type=MESH,
            ).start()
            return 0

        lax.fori_loop(0, n - 1, one, 0)
        r[pl.ds(k * each, each), pl.ds(pl.multiple_of(me_r * ys, ys), ys), :] = s[
            pl.ds(k * per + me_r * each, each)
        ]

    for at, (first, count) in enumerate(groups):
        transform_x(first, count)
        if at == 0:
            pl.semaphore_wait(barrier, n + m - 2)
        for k in range(first, first + count):
            send_rows(k)

    for load in loads[2:]:
        load.wait()

    def upright(row_ref, into):
        size = row_ref.shape[1]
        here = lax.broadcasted_iota(jnp.int32, (size, size), 0)
        there = lax.broadcasted_iota(jnp.int32, (size, size), 1)
        kept = jnp.where(here == there, row_ref[...], 0.0)
        into[...] = jnp.broadcast_to(jnp.sum(kept, axis=1, keepdims=True), into.shape)

    upright(vx, colx)
    upright(vy, coly)
    x_share = r.shape[0]
    part_y = coly[pl.ds(pl.multiple_of(me_c * yc, yc), yc), :]

    def factor(i, _):
        symbol = part_y + colx[pl.ds(me_r * x_share + i, 1), :]
        for at in range(0, vz.shape[1], 128):
            full = symbol + vz[:, at : at + 128]
            f[pl.ds(pl.multiple_of(i * yc, yc), yc), at : at + 128] = (1.0 - 0.2 * full) / (
                1.0 + 0.2 * full
            )
        return 0

    lax.fori_loop(0, x_share, factor, 0)

    def got_rows(k):
        waited = r.at[pl.ds(k * each, each), pl.ds(0, (n - 1) * ys), :]
        pltpu.make_async_copy(waited, waited, recv_r.at[k]).wait()

    def transform_y(k):
        got = jnp.concatenate([r[k * each + j] for j in range(each)], axis=1)
        for b in range(ty.shape[0] // (2 * block)):
            now = from_left(ty[2 * b * block : 2 * (b + 1) * block], got)
            for q in range(block // yc):
                for j in range(each):
                    y[k, b * (block // yc) + q, j] = now[
                        q * yc : (q + 1) * yc, j * zs : (j + 1) * zs
                    ]

    def send_cols(k):
        def one(i, _):
            to = lax.rem(me_c + i, m)
            pltpu.make_async_remote_copy(
                src_ref=y.at[k, to],
                dst_ref=c.at[k, me_c],
                send_sem=send_c.at[k],
                recv_sem=recv_c.at[k],
                device_id={"col": to},
                device_id_type=MESH,
            ).start()
            return 0

        lax.fori_loop(1, m, one, 0)
        c[k, me_c] = y[k, me_c]

    def got_cols(k):
        waited = c.at[k, pl.ds(0, m - 1)]
        pltpu.make_async_copy(waited, waited, recv_c.at[k]).wait()

    def transform_z(k):
        rows = each * yc
        got = jnp.concatenate([c[k, q].reshape(rows, zs) for q in range(m)], axis=1)
        high, low = halves(got)
        both = dot(jnp.concatenate([high, low], axis=0), tzh[...])
        full = both[:rows] + both[rows:] + dot(high, tzl[...])
        at = pl.ds(pl.multiple_of(k * rows, rows), rows)
        out[at, :] = full * f[at, :]

    def step(k, _):
        got_rows(k)
        transform_y(k)
        send_cols(k)

        @pl.when(k >= lag)
        def _():
            got_cols(k - lag)
            transform_z(k - lag)

        return 0

    lax.fori_loop(0, pieces, step, 0)
    def drain(k, _):
        got_cols(k)
        transform_z(k)
        return 0

    lax.fori_loop(pieces - lag, pieces, drain, 0)

    def finish(k, _):
        sent = s.at[pl.ds(0, (n - 1) * each)]
        pltpu.make_async_copy(sent, sent, send_r.at[k]).wait()
        sent = y.at[k, pl.ds(0, m - 1)]
        pltpu.make_async_copy(sent, sent, send_c.at[k]).wait()
        return 0

    lax.fori_loop(0, pieces, finish, 0)


def per_device(n, m, tracer, symbol_x, symbol_y, symbol_z):
    depth, ys, zs = tracer.shape
    height, length = ys * n, zs * m
    x_share, yc = depth // n, height // m
    pieces = min(PIECES, x_share)
    each = x_share // pieces
    per = n * each
    block = min(height, 128)

    groups = [(0, 1)]
    most = max(1, 128 // per)
    while sum(groups[-1]) < pieces:
        first = sum(groups[-1])
        groups.append((first, min(most, pieces - first)))
    order = np.arange(depth).reshape(n, pieces, each).transpose(1, 0, 2).reshape(pieces, per)
    high, low = table_halves(depth)
    tab_x = []
    for first, count in groups:
        rows = order[first : first + count].reshape(-1)
        tab_x += [high[rows], low[rows]]
    tab_x = np.concatenate(tab_x)
    high, low = table_halves(height)
    tab_y = []
    for b in range(0, height, block):
        tab_y += [high[b : b + block], low[b : b + block]]
    tab_y = np.concatenate(tab_y)
    tab_zh, tab_zl = table_halves(length)

    anywhere = pl.BlockSpec(memory_space=pl.ANY)
    dma = pltpu.SemaphoreType.DMA
    out = pl.pallas_call(
        functools.partial(kernel, n, m, pieces, groups, block),
        out_shape=pltpu.VMEM((x_share * yc, length), F32),
        in_specs=[anywhere] * 8,
        out_specs=pl.BlockSpec(memory_space=pltpu.VMEM),
        scratch_shapes=[
            pltpu.VMEM((depth, ys, zs), F32),
            pltpu.VMEM((depth, ys, zs), F32),
            pltpu.VMEM((x_share, height, zs), F32),
            pltpu.VMEM((pieces, m, each, yc, zs), F32),
            pltpu.VMEM((pieces, m, each, yc, zs), F32),
            pltpu.VMEM((x_share * yc, length), F32),
            pltpu.VMEM(tab_x.shape, BF16),
            pltpu.VMEM(tab_y.shape, BF16),
            pltpu.VMEM(tab_zh.shape, BF16),
            pltpu.VMEM(tab_zl.shape, BF16),
            pltpu.VMEM((depth, 128), F32),
            pltpu.VMEM((height, 128), F32),
            pltpu.VMEM((1, depth), F32),
            pltpu.VMEM((1, height), F32),
            pltpu.VMEM((1, length), F32),
            dma((8,)),
            dma((1,)),
            dma((pieces,)),
            dma((pieces,)),
            dma((pieces,)),
            dma((pieces,)),
        ],
        compiler_params=pltpu.CompilerParams(
            collective_id=0,
            has_side_effects=True,
            vmem_limit_bytes=(58 << 20) - 12 * x_share * yc * length,
        ),
    )(
        tracer,
        jnp.asarray(tab_x),
        jnp.asarray(tab_y),
        jnp.asarray(tab_zh),
        jnp.asarray(tab_zl),
        symbol_x[None],
        symbol_y[None],
        symbol_z[None],
    )
    return out.reshape(x_share, yc, length)


def solution(mesh):
    in_specs = (P(None, "row", "col"), P(), P(), P())
    out_specs = P("row", "col", None)
    body = functools.partial(per_device, mesh.shape["row"], mesh.shape["col"])
    return jax.shard_map(
        body, mesh=mesh, in_specs=in_specs, out_specs=out_specs, check_vma=False
    )
```

profile of v0, /device:TPU:0, one launch (start us, length us, event | category | flops | bytes accessed | tf_op | source)
XLA Modules:
  0.0 34.3 jit_solution(5731421183728547542)
XLA Ops:
  0.0 33.3 %shard_map.82 = f32[512,512]{1,0:T(8,128)S(1)} custom-call(f32[128,16,128]{2,1,0:T(8,128)} %field.1, bf16[256,128]{1,0:T(8,128)(2,1)} %constant.8.clone.tab_x, bf16[256,128]{1,0:T(8,128)(2,1)} %constant.9.clone.tab_y, bf16[512,512]{1,0:T(8,128)(2,1)} %constant.10.clone.tab_zh, bf16[512,512]{1,0:T(8,128)(2,1)} %constant.11.clone.tab_zl, f32[1,128]{1,0:T(1,128)} %bitcast.6, ...), custom_call_target="tpu_custom_call" | custom-call | tf_op jit(solution)/shard_map/pallas_call | solution.py:252
  33.3 1.0 %copy.10 = f32[16,32,512]{2,1,0:T(8,128)} copy(f32[16,32,512]{2,1,0:T(8,128)S(1)} %bitcast.4) | data formatting | bytes 2097152
where the time goes:
time: 34.5 us; the launch traced here: 34.3 us
  Pallas kernels  33.3 us (97%)
  local copies, waits for them, and re-layouts  0.97 us (3%)
    pallas_call x1, Pallas kernels, per_device(): pl.pallas_call(functools.partial(kernel, n, m, pieces, groups, block), ou...  33.3 us
    unnamed x1, local copies, waits for them, and re-layouts  0.97 us

commit v1 on v0

v1 whole, which is shorter than its diff:
```python
import functools

import jax
import jax.numpy as jnp
import ml_dtypes
import numpy as np
from jax import lax
from jax.experimental import pallas as pl
from jax.experimental.pallas import tpu as pltpu
from jax.sharding import PartitionSpec as P

MESH = pl.DeviceIdType.MESH
F32 = jnp.float32
BF16 = jnp.bfloat16
LAG = 1


def table_halves(count):
    rank = np.arange(1, count + 1)
    turns = np.outer(rank, rank) % (2 * count + 2)
    table = np.sin(np.pi / (count + 1) * turns) * np.sqrt(2.0 / (count + 1))
    high = table.astype(ml_dtypes.bfloat16)
    low = (table - high.astype(np.float64)).astype(ml_dtypes.bfloat16)
    return high, low


def left_table(high, low):
    return np.concatenate(
        [np.concatenate([high, high], axis=1), np.concatenate([low, 0 * low], axis=1)]
    )


def halves(values):
    high = values.astype(BF16)
    return high, (values - high.astype(F32)).astype(BF16)


def dot(a, b):
    return jnp.dot(a, b, preferred_element_type=F32)


def from_left(table, values):
    rows = table.shape[0] // 2
    both = dot(table, jnp.concatenate(halves(values), axis=0))
    return both[:rows] + both[rows:]


def piece_sizes(share):
    size = max(1, share // 4)
    sizes = []
    left = share
    while left:
        size = min(size, left)
        if left <= size:
            size = max(1, left // 2)
        sizes.append(size)
        left -= size
    return sizes


def kernel(
    n, m, sizes, groups, block,
    field, tab_x, tab_y, tab_zh, tab_zl, sx, sy, sz, out,
    d, s, r, y, c, f, tx, ty, tzh, tzl, colx, coly, vx, vy, vz,
    in_sem, send_r, recv_r, send_c, recv_c, up_r, up_c,
):
    pieces = len(sizes)
    starts = [sum(sizes[:k]) for k in range(pieces)]
    lag = min(LAG, pieces)
    me_r, me_c = lax.axis_index("row"), lax.axis_index("col")
    depth, ys, zs = d.shape
    yc = y.shape[1]
    loads = [(field, d, 0), (tab_x, tx, 1), (tab_y, ty, 2), (tab_zh, tzh, 3), (tab_zl, tzl, 4)]
    loads += [(sx, vx, 5), (sy, vy, 6), (sz, vz, 7)]
    loads = [pltpu.make_async_copy(a, b, in_sem.at[i]) for a, b, i in loads]

    odd = lax.rem(me_r, 2)
    tier = lax.div(me_r, 2)
    tiers = n // 2
    barrier = pltpu.get_barrier_semaphore()
    flip = 1 if m % 2 == 0 else 0
    place = lambda at: at ^ flip

    def greet_row(to, _):
        @pl.when(jnp.logical_or(odd == 0, lax.rem(to, 2) == 1))
        def _():
            pl.semaphore_signal(barrier, inc=1, device_id={"row": to}, device_id_type=MESH)

        return 0

    def greet_col(at, _):
        pl.semaphore_signal(barrier, inc=1, device_id={"col": place(at)}, device_id_type=MESH)
        return 0

    lax.fori_loop(me_r + 1, n, greet_row, 0)
    lax.fori_loop(place(me_c) + 1, m, greet_col, 0)
    for load in loads:
        load.start()
    earlier = jnp.where(odd == 1, me_r, tier) + place(me_c)

    @pl.when(earlier > 0)
    def _():
        pl.semaphore_wait(barrier, earlier)

    @pl.when(odd == 1)
    def _():
        def answer(to, _):
            pl.semaphore_signal(
                up_r.at[tier], inc=1, device_id={"row": to}, device_id_type=MESH
            )
            return 0

        lax.fori_loop(0, me_r, answer, 0)

    def answer_col(at, _):
        pl.semaphore_signal(up_c, inc=1, device_id={"col": place(at)}, device_id_type=MESH)
        return 0

    lax.fori_loop(0, place(me_c), answer_col, 0)

    loads[0].wait()
    loads[1].wait()
    lanes = d.reshape(depth * ys, zs)
    modes = s.reshape(s.shape[0] * ys, zs)

    def transform_x(first, count):
        begin = n * starts[first]
        rows = n * sum(sizes[first : first + count])
        table = tx[2 * begin : 2 * (begin + rows)]

        def pair(i, _):
            got = jnp.concatenate(
                [lanes[pl.ds(2 * i + h, depth, stride=ys), :] for h in range(2)], axis=1
            )
            got = from_left(table, got)
            for h in range(2):
                modes[pl.ds(begin * ys + 2 * i + h, rows, stride=ys), :] = got[
                    :, h * zs : (h + 1) * zs
                ]
            return 0

        lax.fori_loop(0, ys // 2, pair, 0, unroll=True)

    mine = pl.ds(pl.multiple_of(me_r * ys, ys), ys)

    def send_row(k, to):
        each = sizes[k]
        pltpu.make_async_remote_copy(
            src_ref=s.at[pl.ds(n * starts[k] + to * each, each)],
            dst_ref=r.at[pl.ds(starts[k], each), mine, :],
            send_sem=send_r.at[k],
            recv_sem=recv_r.at[k],
            device_id={"row": to},
            device_id_type=MESH,
        ).start()

    def keep_row(k):
        each = sizes[k]
        r[pl.ds(starts[k], each), mine, :] = s[pl.ds(n * starts[k] + me_r * each, each)]

    def send_rows(k):
        def one(i, _):
            send_row(k, lax.rem(me_r + 1 + i, n))
            return 0

        lax.fori_loop(0, n - 1, one, 0)
        keep_row(k)

    def wait_up(at):
        pl.semaphore_wait(up_r.at[at], 1)

    def first_rows(k):
        @pl.when(odd == 0)
        def _():
            wait_up(tier)

        def low(to, _):
            @pl.when(to != me_r)
            def _():
                send_row(k, to)

            return 0

        lax.fori_loop(0, 2 * tier + 2, low, 0)

    def later_rows(k):
        def late(at, _):
            wait_up(at)
            for h in range(2):
                send_row(k, 2 * at + h)
            return 0

        lax.fori_loop(tier + 1, tiers, late, 0)
        keep_row(k)

    for at, (first, count) in enumerate(groups):
        transform_x(first, count)
        if at == 0:
            first_rows(0)
        if at == min(1, len(groups) - 1):
            later_rows(0)
        for k in range(max(1, first), first + count):
            send_rows(k)

    for load in loads[2:]:
        load.wait()

    def upright(row_ref, into):
        size = row_ref.shape[1]
        here = lax.broadcasted_iota(jnp.int32, (size, size), 0)
        there = lax.broadcasted_iota(jnp.int32, (size, size), 1)
        kept = jnp.where(here == there, row_ref[...], 0.0)
        into[...] = jnp.broadcast_to(jnp.sum(kept, axis=1, keepdims=True), into.shape)

    upright(vx, colx)
    upright(vy, coly)
    x_share = r.shape[0]
    part_y = coly[pl.ds(pl.multiple_of(me_c * yc, yc), yc), :]

    def factor(i, _):
        symbol = part_y + colx[pl.ds(me_r * x_share + i, 1), :]
        for at in range(0, vz.shape[1], 128):
            full = symbol + vz[:, at : at + 128]
            f[pl.ds(pl.multiple_of(i * yc, yc), yc), at : at + 128] = (1.0 - 0.2 * full) / (
                1.0 + 0.2 * full
            )
        return 0

    lax.fori_loop(0, x_share, factor, 0)

    @pl.when(place(me_c) < m - 1)
    def _():
        pl.semaphore_wait(up_c, m - 1 - place(me_c))

    def got_rows(k):
        waited = r.at[pl.ds(starts[k], sizes[k]), pl.ds(0, (n - 1) * ys), :]
        pltpu.make_async_copy(waited, waited, recv_r.at[k]).wait()

    def transform_y(k):
        each, base = sizes[k], m * starts[k]
        got = jnp.concatenate([r[starts[k] + j] for j in range(each)], axis=1)
        for b in range(ty.shape[0] // (2 * block)):
            now = from_left(ty[2 * b * block : 2 * (b + 1) * block], got)
            for q in range(block // yc):
                for j in range(each):
                    y[base + (b * (block // yc) + q) * each + j] = now[
                        q * yc : (q + 1) * yc, j * zs : (j + 1) * zs
                    ]

    def send_cols(k):
        each, base = sizes[k], m * starts[k]

        def one(i, _):
            to = lax.rem(me_c + i, m)
            pltpu.make_async_remote_copy(
                src_ref=y.at[pl.ds(base + to * each, each)],
                dst_ref=c.at[pl.ds(base + me_c * each, each)],
                send_sem=send_c.at[k],
                recv_sem=recv_c.at[k],
                device_id={"col": to},
                device_id_type=MESH,
            ).start()
            return 0

        lax.fori_loop(1, m, one, 0)
        own = pl.ds(base + me_c * each, each)
        c[own] = y[own]

    def got_cols(k):
        waited = c.at[pl.ds(m * starts[k], (m - 1) * sizes[k])]
        pltpu.make_async_copy(waited, waited, recv_c.at[k]).wait()

    def transform_z(k):
        each, base = sizes[k], m * starts[k]
        rows = each * yc
        got = jnp.concatenate(
            [c[base + q * each : base + (q + 1) * each].reshape(rows, zs) for q in range(m)],
            axis=1,
        )
        high, low = halves(got)
        both = dot(jnp.concatenate([high, low], axis=0), tzh[...])
        full = both[:rows] + both[rows:] + dot(high, tzl[...])
        at = slice(starts[k] * yc, starts[k] * yc + rows)
        out[at, :] = full * f[at, :]

    for k in range(pieces):
        got_rows(k)
        transform_y(k)
        send_cols(k)
        if k >= lag:
            got_cols(k - lag)
            transform_z(k - lag)
    for k in range(pieces - lag, pieces):
        got_cols(k)
        transform_z(k)

    for k in range(pieces):
        sent = s.at[pl.ds(0, (n - 1) * sizes[k])]
        pltpu.make_async_copy(sent, sent, send_r.at[k]).wait()
        sent = y.at[pl.ds(0, (m - 1) * sizes[k])]
        pltpu.make_async_copy(sent, sent, send_c.at[k]).wait()


def per_device(n, m, tracer, symbol_x, symbol_y, symbol_z):
    depth, ys, zs = tracer.shape
    height, length = ys * n, zs * m
    x_share, yc = depth // n, height // m
    sizes = piece_sizes(x_share)
    pieces = len(sizes)
    starts = [sum(sizes[:k]) for k in range(pieces)]
    block = min(height, 128)

    groups = [(0, 1)]
    while sum(groups[-1]) < pieces:
        first = sum(groups[-1])
        count = 1
        while first + count < pieces and n * sum(sizes[first : first + count + 1]) <= 128:
            count += 1
        groups.append((first, count))
    share = np.arange(depth).reshape(n, x_share)
    order = [share[:, a : a + e].reshape(-1) for a, e in zip(starts, sizes)]
    high, low = table_halves(depth)
    tab_x = []
    for first, count in groups:
        rows = np.concatenate(order[first : first + count])
        tab_x.append(left_table(high[rows], low[rows]))
    tab_x = np.concatenate(tab_x)
    high, low = table_halves(height)
    tab_y = [left_table(high[b : b + block], low[b : b + block]) for b in range(0, height, block)]
    tab_y = np.concatenate(tab_y)
    tab_zh, tab_zl = table_halves(length)

    anywhere = pl.BlockSpec(memory_space=pl.ANY)
    dma = pltpu.SemaphoreType.DMA
    regular = pltpu.SemaphoreType.REGULAR
    out = pl.pallas_call(
        functools.partial(kernel, n, m, sizes, groups, block),
        out_shape=pltpu.VMEM((x_share * yc, length), F32),
        in_specs=[anywhere] * 8,
        out_specs=pl.BlockSpec(memory_space=pltpu.VMEM),
        scratch_shapes=[
            pltpu.VMEM((depth, ys, zs), F32),
            pltpu.VMEM((depth, ys, zs), F32),
            pltpu.VMEM((x_share, height, zs), F32),
            pltpu.VMEM((m * x_share, yc, zs), F32),
            pltpu.VMEM((m * x_share, yc, zs), F32),
            pltpu.VMEM((x_share * yc, length), F32),
            pltpu.VMEM(tab_x.shape, BF16),
            pltpu.VMEM(tab_y.shape, BF16),
            pltpu.VMEM(tab_zh.shape, BF16),
            pltpu.VMEM(tab_zl.shape, BF16),
            pltpu.VMEM((depth, 128), F32),
            pltpu.VMEM((height, 128), F32),
            pltpu.VMEM((1, depth), F32),
            pltpu.VMEM((1, height), F32),
            pltpu.VMEM((1, length), F32),
            dma((8,)),
            dma((pieces,)),
            dma((pieces,)),
            dma((pieces,)),
            dma((pieces,)),
            regular((n // 2,)),
            regular,
        ],
        compiler_params=pltpu.CompilerParams(
            collective_id=0,
            has_side_effects=True,
            vmem_limit_bytes=(58 << 20) - 12 * x_share * yc * length,
        ),
    )(
        tracer,
        jnp.asarray(tab_x),
        jnp.asarray(tab_y),
        jnp.asarray(tab_zh),
        jnp.asarray(tab_zl),
        symbol_x[None],
        symbol_y[None],
        symbol_z[None],
    )
    return out.reshape(x_share, yc, length)


def solution(mesh):
    in_specs = (P(None, "row", "col"), P(), P(), P())
    out_specs = P("row", "col", None)
    body = functools.partial(per_device, mesh.shape["row"], mesh.shape["col"])
    return jax.shard_map(
        body, mesh=mesh, in_specs=in_specs, out_specs=out_specs, check_vma=False
    )
```

time: 34.5 us -> 36.4 us (1.055)
  Pallas kernels: 33.3 us -> 35.3 us
    pallas_call x1, Pallas kernels: 33.3 us -> 35.3 us  [per_device(): pl.pallas_call(functools.partial(kernel, n, m, sizes, groups, block), out...]
where the time goes in v1:
time: 36.4 us; the launch traced here: 36.3 us
  Pallas kernels  35.3 us (97%)
  local copies, waits for them, and re-layouts  0.97 us (3%)
    pallas_call x1, Pallas kernels, per_device(): pl.pallas_call(functools.partial(kernel, n, m, sizes, groups, block), out...  35.3 us
    unnamed x1, local copies, waits for them, and re-layouts  0.97 us

profile of v1, /device:TPU:0, one launch (start us, length us, event | category | flops | bytes accessed | tf_op | source)
XLA Modules:
  0.0 36.3 jit_solution(2371384912237881960)
XLA Ops:
  0.0 35.3 %shard_map.82 = f32[512,512]{1,0:T(8,128)S(1)} custom-call(f32[128,16,128]{2,1,0:T(8,128)} %field.1, bf16[256,256]{1,0:T(8,128)(2,1)} %constant.8.clone.tab_x, bf16[256,256]{1,0:T(8,128)(2,1)} %constant.9.clone.tab_y, bf16[512,512]{1,0:T(8,128)(2,1)} %constant.10.clone.tab_zh, bf16[512,512]{1,0:T(8,128)(2,1)} %constant.11.clone.tab_zl, f32[1,128]{1,0:T(1,128)} %bitcast.6, ...), custom_call_target="tpu_custom_call" | custom-call | tf_op jit(solution)/shard_map/pallas_call | solution.py:336
  35.3 1.0 %copy.10 = f32[16,32,512]{2,1,0:T(8,128)} copy(f32[16,32,512]{2,1,0:T(8,128)S(1)} %bitcast.4) | data formatting | bytes 2097152

commit v2 on v1

--- a/solution.py
+++ b/solution.py
@@ -12,7 +12,14 @@
 MESH = pl.DeviceIdType.MESH
 F32 = jnp.float32
 BF16 = jnp.bfloat16
-LAG = 1
+PIECES = 8
+LEAD = 1
+OWN = 6
+OWN_B = 3
+BEGUN = 4
+BEGUN_LOW = 5
+LAG = 5
+CUTS = 1
 
 
 def table_halves(count):
@@ -46,7 +53,7 @@
 
 
 def piece_sizes(share):
-    size = max(1, share // 4)
+    size = max(1, share // PIECES)
     sizes = []
     left = share
     while left:
@@ -61,16 +68,22 @@
 def kernel(
     n, m, sizes, groups, block,
     field, tab_x, tab_y, tab_zh, tab_zl, sx, sy, sz, out,
-    d, s, r, y, c, f, tx, ty, tzh, tzl, colx, coly, vx, vy, vz,
-    in_sem, send_r, recv_r, send_c, recv_c, up_r, up_c,
+    d, s, r, y, c, f, pass_on, tx, ty, tzh, tzl, colx, coly, vx, vy, vz,
+    in_sem, send_r, recv_r, send_c, recv_c, recv_p, up_r, up_c,
 ):
     pieces = len(sizes)
     starts = [sum(sizes[:k]) for k in range(pieces)]
-    lag = min(LAG, pieces)
+    lag, lead = min(LAG, pieces), min(LEAD, pieces - 1)
     me_r, me_c = lax.axis_index("row"), lax.axis_index("col")
     depth, ys, zs = d.shape
     yc = y.shape[1]
-    loads = [(field, d, 0), (tab_x, tx, 1), (tab_y, ty, 2), (tab_zh, tzh, 3), (tab_zl, tzl, 4)]
+    cut = ys // CUTS
+    fields = [pl.ds(i * cut, cut) for i in range(CUTS)]
+    fields = [
+        pltpu.make_async_copy(field.at[:, at, :], d.at[:, at, :], in_sem.at[8 + i])
+        for i, at in enumerate(fields)
+    ]
+    loads = [(tab_x, tx, 1), (tab_y, ty, 2), (tab_zh, tzh, 3), (tab_zl, tzl, 4)]
     loads += [(sx, vx, 5), (sy, vy, 6), (sz, vz, 7)]
     loads = [pltpu.make_async_copy(a, b, in_sem.at[i]) for a, b, i in loads]
 
@@ -94,7 +107,7 @@
 
     lax.fori_loop(me_r + 1, n, greet_row, 0)
     lax.fori_loop(place(me_c) + 1, m, greet_col, 0)
-    for load in loads:
+    for load in loads[:1] + fields + loads[1:]:
         load.start()
     earlier = jnp.where(odd == 1, me_r, tier) + place(me_c)
 
@@ -119,7 +132,6 @@
     lax.fori_loop(0, place(me_c), answer_col, 0)
 
     loads[0].wait()
-    loads[1].wait()
     lanes = d.reshape(depth * ys, zs)
     modes = s.reshape(s.shape[0] * ys, zs)
 
@@ -139,15 +151,19 @@
                 ]
             return 0
 
-        lax.fori_loop(0, ys // 2, pair, 0, unroll=True)
-
-    mine = pl.ds(pl.multiple_of(me_r * ys, ys), ys)
+        for i in range(CUTS):
+            if first == 0:
+                fields[i].wait()
+            lax.fori_loop(i * cut // 2, (i + 1) * cut // 2, pair, 0, unroll=True)
+
+    def rows_of(at):
+        return pl.ds(pl.multiple_of(at * ys, ys), ys)
 
     def send_row(k, to):
         each = sizes[k]
         pltpu.make_async_remote_copy(
             src_ref=s.at[pl.ds(n * starts[k] + to * each, each)],
-            dst_ref=r.at[pl.ds(starts[k], each), mine, :],
+            dst_ref=r.at[pl.ds(starts[k], each), rows_of(me_r), :],
             send_sem=send_r.at[k],
             recv_sem=recv_r.at[k],
             device_id={"row": to},
@@ -156,53 +172,194 @@
 
     def keep_row(k):
         each = sizes[k]
-        r[pl.ds(starts[k], each), mine, :] = s[pl.ds(n * starts[k] + me_r * each, each)]
-
-    def send_rows(k):
-        def one(i, _):
-            send_row(k, lax.rem(me_r + 1 + i, n))
-            return 0
-
-        lax.fori_loop(0, n - 1, one, 0)
-        keep_row(k)
+        r[pl.ds(starts[k], each), rows_of(me_r), :] = s[pl.ds(n * starts[k] + me_r * each, each)]
 
     def wait_up(at):
         pl.semaphore_wait(up_r.at[at], 1)
 
-    def first_rows(k):
+    half, step_out = tiers // 2, tiers // 4
+    high = tier >= half
+    low = jnp.logical_not(high)
+    outer = jnp.logical_or(tier < step_out, tier >= tiers - step_out)
+    inner = jnp.logical_not(outer)
+    far, near = jnp.where(high, 0, half), jnp.where(high, half, 0)
+    behind = jnp.where(high, me_r + 2 * step_out, me_r - 2 * step_out)
+    ahead = jnp.where(high, me_r - 2 * step_out, me_r + 2 * step_out)
+    every = range(pieces)
+
+    def send_tier(k, at, other):
+        send_row(k, 2 * at + (odd ^ other))
+
+    def send_tiers(ks, begin, end, wait=False):
+        def one(at, _):
+            if wait:
+                wait_up(at)
+            for k in ks:
+                for other in range(2):
+                    send_row(k, 2 * at + other)
+            return 0
+
+        lax.fori_loop(begin, end, one, 0)
+
+    def hand_on(k):
+        each = sizes[k]
+        pltpu.make_async_remote_copy(
+            src_ref=s.at[pl.ds(n * starts[k] + 2 * far * each, n // 2 * each)],
+            dst_ref=pass_on.at[pl.ds(n // 2 * starts[k], n // 2 * each)],
+            send_sem=send_r.at[k],
+            recv_sem=recv_p.at[k],
+            device_id={"row": ahead},
+            device_id_type=MESH,
+        ).start()
+
+    def got_pass(k):
+        waited = pass_on.at[pl.ds(n // 2 * starts[k], n // 2 * sizes[k])]
+        pltpu.make_async_copy(waited, waited, recv_p.at[k]).wait()
+
+    def pass_rows(k, begin, end):
+        each = sizes[k]
+
+        def one(to, _):
+            pltpu.make_async_remote_copy(
+                src_ref=pass_on.at[pl.ds(n // 2 * starts[k] + (to - 2 * far) * each, each)],
+                dst_ref=r.at[pl.ds(starts[k], each), rows_of(behind), :],
+                send_sem=send_r.at[k],
+                recv_sem=recv_r.at[k],
+                device_id={"row": to},
+                device_id_type=MESH,
+            ).start()
+            return 0
+
+        lax.fori_loop(begin, end, one, 0)
+
+    def own_rows(k, begin, end):
+        def one(to, _):
+            send_row(k, to)
+            return 0
+
+        lax.fori_loop(begin, end, one, 0)
+
+    def hear_peer():
         @pl.when(odd == 0)
         def _():
             wait_up(tier)
 
-        def low(to, _):
-            @pl.when(to != me_r)
+    def start_far():
+        for other in range(2):
+            if other == 1:
+                hear_peer()
+
+            def one(at, _):
+                send_tier(0, at, other)
+                return 0
+
+            lax.fori_loop(0, half, one, 0)
+
+    def send_peer():
+        for k in every:
+            send_tier(k, tier, 1)
+
+    begin, turn, end = 2 * far, jnp.where(high, 1, n), jnp.where(high, n // 2, n)
+
+    def by_core(act):
+        for core, own in enumerate((OWN, OWN_B)):
+
+            @pl.when(lax.rem(me_c, 2) == core)
             def _():
-                send_row(k, to)
-
-            return 0
-
-        lax.fori_loop(0, 2 * tier + 2, low, 0)
-
-    def later_rows(k):
-        def late(at, _):
-            wait_up(at)
-            for h in range(2):
-                send_row(k, 2 * at + h)
-            return 0
-
-        lax.fori_loop(tier + 1, tiers, late, 0)
-        keep_row(k)
+                act(min(own, pieces))
+
+    def cross(step, own):
+        def part(step, begin, end):
+            if 0 <= step < pieces:
+                pass_rows(step, begin, end)
+            for k in range(own, pieces):
+                if k - max(1, 2 * own - 1 - k) == step:
+                    own_rows(k, begin, end)
+
+        if step < pieces:
+            got_pass(step)
+            part(step, begin, turn)
+        if 0 <= step - lead:
+            part(step - lead, turn, end)
 
     for at, (first, count) in enumerate(groups):
         transform_x(first, count)
         if at == 0:
-            first_rows(0)
-        if at == min(1, len(groups) - 1):
-            later_rows(0)
-        for k in range(max(1, first), first + count):
-            send_rows(k)
-
-    for load in loads[2:]:
+
+            @pl.when(jnp.logical_and(high, inner))
+            def _():
+                start_far()
+
+            @pl.when(jnp.logical_and(high, outer))
+            def _():
+                hand_on(0)
+
+    begun_high, begun_low = min(BEGUN, pieces), min(BEGUN_LOW, pieces)
+
+    @pl.when(jnp.logical_and(high, inner))
+    def _():
+        by_core(lambda own: [send_tiers([k], far, far + half) for k in range(1, own)])
+        send_peer()
+        send_tiers(every, tier + 1, tiers, wait=True)
+
+    @pl.when(jnp.logical_and(low, inner))
+    def _():
+        hear_peer()
+        send_tiers(every, 0, tier)
+        send_peer()
+        for at in range(half, tiers):
+            wait_up(at)
+            by_core(lambda own: send_tiers(range(own), at, at + 1))
+
+    @pl.when(jnp.logical_and(high, outer))
+    def _():
+        hear_peer()
+        for k in every:
+            if k:
+                hand_on(k)
+            send_tiers([k], half, tier)
+        send_peer()
+        send_tiers(every, tier + 1, tiers, wait=True)
+
+    @pl.when(jnp.logical_and(low, outer))
+    def _():
+        hear_peer()
+        send_peer()
+        send_tiers(every, 0, tier)
+
+        def one(at, _):
+            wait_up(at)
+            return 0
+
+        lax.fori_loop(tier + 1, half, one, 0)
+        for k in every:
+            hand_on(k)
+            send_tiers([k], tier + 1, half)
+
+    def crosses(steps):
+        by_core(lambda own: [cross(step, own) for step in steps])
+
+    def steps_from(step):
+        return [at for at in range(step, pieces + lead) if at == step or step == pieces - 1] * (
+            step < pieces
+        )
+
+    inner_high, inner_low = jnp.logical_and(high, inner), jnp.logical_and(low, inner)
+
+    @pl.when(inner_high)
+    def _():
+        for step in range(begun_high):
+            crosses(steps_from(step))
+
+    @pl.when(inner_low)
+    def _():
+        for step in range(begun_low):
+            crosses(steps_from(step))
+
+    for k in every:
+        keep_row(k)
+
+    for load in loads[1:]:
         load.wait()
 
     def upright(row_ref, into):
@@ -285,20 +442,45 @@
 
     for k in range(pieces):
         got_rows(k)
+        for which, begun in ((inner_high, begun_high), (inner_low, begun_low)):
+            steps = steps_from(k + begun)
+            if steps:
+
+                @pl.when(which)
+                def _():
+                    crosses(steps)
+
         transform_y(k)
         send_cols(k)
         if k >= lag:
             got_cols(k - lag)
             transform_z(k - lag)
+    def sent_rows(k):
+        @pl.when(inner)
+        def _():
+            sent = pass_on.at[pl.ds(0, n // 2 * sizes[k])]
+            pltpu.make_async_copy(sent, sent, send_r.at[k]).wait()
+
+        sent = s.at[pl.ds(0, (n - 1) * sizes[k])]
+        pltpu.make_async_copy(sent, sent, send_r.at[k]).wait()
+
+    def sent_cols(k):
+        sent = y.at[pl.ds(0, (m - 1) * sizes[k])]
+        pltpu.make_async_copy(sent, sent, send_c.at[k]).wait()
+
     for k in range(pieces - lag, pieces):
+        if k == pieces - 1:
+            for j in every:
+                sent_rows(j)
+                sent_cols(j)
+
+            @pl.when(jnp.logical_and(low, outer))
+            def _():
+                for at in range(half, tiers):
+                    wait_up(at)
+
         got_cols(k)
         transform_z(k)
-
-    for k in range(pieces):
-        sent = s.at[pl.ds(0, (n - 1) * sizes[k])]
-        pltpu.make_async_copy(sent, sent, send_r.at[k]).wait()
-        sent = y.at[pl.ds(0, (m - 1) * sizes[k])]
-        pltpu.make_async_copy(sent, sent, send_c.at[k]).wait()
 
 
 def per_device(n, m, tracer, symbol_x, symbol_y, symbol_z):
@@ -345,6 +527,7 @@
             pltpu.VMEM((m * x_share, yc, zs), F32),
             pltpu.VMEM((m * x_share, yc, zs), F32),
             pltpu.VMEM((x_share * yc, length), F32),
+            pltpu.VMEM((n // 2 * x_share, ys, zs), F32),
             pltpu.VMEM(tab_x.shape, BF16),
             pltpu.VMEM(tab_y.shape, BF16),
             pltpu.VMEM(tab_zh.shape, BF16),
@@ -354,7 +537,8 @@
             pltpu.VMEM((1, depth), F32),
             pltpu.VMEM((1, height), F32),
             pltpu.VMEM((1, length), F32),
-            dma((8,)),
+            dma((8 + CUTS,)),
+            dma((pieces,)),
             dma((pieces,)),
             dma((pieces,)),
             dma((pieces,)),

time: 36.4 us -> 34.2 us (0.940)
  Pallas kernels: 35.3 us -> 33.1 us
    pallas_call x1, Pallas kernels: 35.3 us -> 33.1 us  [per_device(): pl.pallas_call(functools.partial(kernel, n, m, sizes, groups, block), out...]
where the time goes in v2:
time: 34.2 us; the launch traced here: 34 us
  Pallas kernels  33.1 us (97%)
  local copies, waits for them, and re-layouts  0.97 us (3%)
    pallas_call x1, Pallas kernels, per_device(): pl.pallas_call(functools.partial(kernel, n, m, sizes, groups, block), out...  33.1 us
    unnamed x1, local copies, waits for them, and re-layouts  0.97 us

profile of v2, /device:TPU:0, one launch (start us, length us, event | category | flops | bytes accessed | tf_op | source)
XLA Modules:
  0.0 34.0 jit_solution(6785798838834652883)
XLA Ops:
  0.0 33.1 %shard_map.82 = f32[512,512]{1,0:T(8,128)S(1)} custom-call(f32[128,16,128]{2,1,0:T(8,128)} %field.1, bf16[256,256]{1,0:T(8,128)(2,1)} %constant.8.clone.tab_x, bf16[256,256]{1,0:T(8,128)(2,1)} %constant.9.clone.tab_y, bf16[512,512]{1,0:T(8,128)(2,1)} %constant.10.clone.tab_zh, bf16[512,512]{1,0:T(8,128)(2,1)} %constant.11.clone.tab_zl, f32[1,128]{1,0:T(1,128)} %bitcast.6, ...), custom_call_target="tpu_custom_call" | custom-call | tf_op jit(solution)/shard_map/pallas_call | solution.py:518
  33.1 1.0 %copy.10 = f32[16,32,512]{2,1,0:T(8,128)} copy(f32[16,32,512]{2,1,0:T(8,128)S(1)} %bitcast.4) | data formatting | bytes 2097152

commit v3 on v2

--- a/solution.py
+++ b/solution.py
@@ -13,13 +13,14 @@
 F32 = jnp.float32
 BF16 = jnp.bfloat16
 PIECES = 8
-LEAD = 1
+LEAD = 2
 OWN = 6
 OWN_B = 3
-BEGUN = 4
-BEGUN_LOW = 5
+BEGUN = 5
+BEGUN_LOW = 6
 LAG = 5
 CUTS = 1
+NEAR_LAG = 5
 
 
 def table_halves(count):
@@ -164,7 +165,7 @@
         pltpu.make_async_remote_copy(
             src_ref=s.at[pl.ds(n * starts[k] + to * each, each)],
             dst_ref=r.at[pl.ds(starts[k], each), rows_of(me_r), :],
-            send_sem=send_r.at[k],
+            send_sem=send_r,
             recv_sem=recv_r.at[k],
             device_id={"row": to},
             device_id_type=MESH,
@@ -185,7 +186,7 @@
     far, near = jnp.where(high, 0, half), jnp.where(high, half, 0)
     behind = jnp.where(high, me_r + 2 * step_out, me_r - 2 * step_out)
     ahead = jnp.where(high, me_r - 2 * step_out, me_r + 2 * step_out)
-    every = range(pieces)
+    every, near_lag = range(pieces), min(NEAR_LAG, pieces)
 
     def send_tier(k, at, other):
         send_row(k, 2 * at + (odd ^ other))
@@ -206,7 +207,7 @@
         pltpu.make_async_remote_copy(
             src_ref=s.at[pl.ds(n * starts[k] + 2 * far * each, n // 2 * each)],
             dst_ref=pass_on.at[pl.ds(n // 2 * starts[k], n // 2 * each)],
-            send_sem=send_r.at[k],
+            send_sem=send_r,
             recv_sem=recv_p.at[k],
             device_id={"row": ahead},
             device_id_type=MESH,
@@ -223,7 +224,7 @@
             pltpu.make_async_remote_copy(
                 src_ref=pass_on.at[pl.ds(n // 2 * starts[k] + (to - 2 * far) * each, each)],
                 dst_ref=r.at[pl.ds(starts[k], each), rows_of(behind), :],
-                send_sem=send_r.at[k],
+                send_sem=send_r,
                 recv_sem=recv_r.at[k],
                 device_id={"row": to},
                 device_id_type=MESH,
@@ -314,10 +315,11 @@
     @pl.when(jnp.logical_and(high, outer))
     def _():
         hear_peer()
-        for k in every:
-            if k:
+        for k in range(pieces + near_lag):
+            if 0 < k < pieces:
                 hand_on(k)
-            send_tiers([k], half, tier)
+            if k >= near_lag:
+                send_tiers([k - near_lag], half, tier)
         send_peer()
         send_tiers(every, tier + 1, tiers, wait=True)
 
@@ -332,9 +334,11 @@
             return 0
 
         lax.fori_loop(tier + 1, half, one, 0)
-        for k in every:
-            hand_on(k)
-            send_tiers([k], tier + 1, half)
+        for k in range(pieces + near_lag):
+            if k < pieces:
+                hand_on(k)
+            if k >= near_lag:
+                send_tiers([k - near_lag], tier + 1, half)
 
     def crosses(steps):
         by_core(lambda own: [cross(step, own) for step in steps])
@@ -412,7 +416,7 @@
             pltpu.make_async_remote_copy(
                 src_ref=y.at[pl.ds(base + to * each, each)],
                 dst_ref=c.at[pl.ds(base + me_c * each, each)],
-                send_sem=send_c.at[k],
+                send_sem=send_c,
                 recv_sem=recv_c.at[k],
                 device_id={"col": to},
                 device_id_type=MESH,
@@ -455,24 +459,21 @@
         if k >= lag:
             got_cols(k - lag)
             transform_z(k - lag)
-    def sent_rows(k):
+    def sent_all():
         @pl.when(inner)
         def _():
-            sent = pass_on.at[pl.ds(0, n // 2 * sizes[k])]
-            pltpu.make_async_copy(sent, sent, send_r.at[k]).wait()
-
-        sent = s.at[pl.ds(0, (n - 1) * sizes[k])]
-        pltpu.make_async_copy(sent, sent, send_r.at[k]).wait()
-
-    def sent_cols(k):
-        sent = y.at[pl.ds(0, (m - 1) * sizes[k])]
-        pltpu.make_async_copy(sent, sent, send_c.at[k]).wait()
+            pltpu.make_async_copy(pass_on, pass_on, send_r).wait()
+
+        sent = s.at[pl.ds(0, (n - 1) * x_share)]
+        pltpu.make_async_copy(sent, sent, send_r).wait()
+
+    def sent_cols():
+        sent = y.at[pl.ds(0, (m - 1) * x_share)]
+        pltpu.make_async_copy(sent, sent, send_c).wait()
 
     for k in range(pieces - lag, pieces):
         if k == pieces - 1:
-            for j in every:
-                sent_rows(j)
-                sent_cols(j)
+            sent_all()
 
             @pl.when(jnp.logical_and(low, outer))
             def _():
@@ -481,6 +482,7 @@
 
         got_cols(k)
         transform_z(k)
+    sent_cols()
 
 
 def per_device(n, m, tracer, symbol_x, symbol_y, symbol_z):
@@ -538,9 +540,9 @@
             pltpu.VMEM((1, height), F32),
             pltpu.VMEM((1, length), F32),
             dma((8 + CUTS,)),
+            dma,
             dma((pieces,)),
-            dma((pieces,)),
-            dma((pieces,)),
+            dma,
             dma((pieces,)),
             dma((pieces,)),
             regular((n // 2,)),

time: 34.2 us -> 32.9 us (0.962); the launches traced: 34 us -> 32.4 us
  Pallas kernels: 33.1 us -> 31.4 us
    pallas_call x1, Pallas kernels: 33.1 us -> 31.4 us  [per_device(): pl.pallas_call(functools.partial(kernel, n, m, sizes, groups, block), out...]
where the time goes in v3:
time: 32.9 us; the launch traced here: 32.4 us
  Pallas kernels  31.4 us (95%)
  local copies, waits for them, and re-layouts  0.97 us (3%)
    pallas_call x1, Pallas kernels, per_device(): pl.pallas_call(functools.partial(kernel, n, m, sizes, groups, block), out...  31.4 us
    unnamed x1, local copies, waits for them, and re-layouts  0.97 us

profile of v3, /device:TPU:0, one launch (start us, length us, event | category | flops | bytes accessed | tf_op | source)
XLA Modules:
  0.0 32.4 jit_solution(5988196920070500522)
XLA Ops:
  0.0 31.4 %shard_map.82 = f32[512,512]{1,0:T(8,128)S(1)} custom-call(f32[128,16,128]{2,1,0:T(8,128)} %field.1, bf16[256,256]{1,0:T(8,128)(2,1)} %constant.8.clone.tab_x, bf16[256,256]{1,0:T(8,128)(2,1)} %constant.9.clone.tab_y, bf16[512,512]{1,0:T(8,128)(2,1)} %constant.10.clone.tab_zh, bf16[512,512]{1,0:T(8,128)(2,1)} %constant.11.clone.tab_zl, f32[1,128]{1,0:T(1,128)} %bitcast.6, ...), custom_call_target="tpu_custom_call" | custom-call | tf_op jit(solution)/shard_map/pallas_call | solution.py:520
  31.4 1.0 %copy.10 = f32[16,32,512]{2,1,0:T(8,128)} copy(f32[16,32,512]{2,1,0:T(8,128)S(1)} %bitcast.4) | data formatting | bytes 2097152

commit v4 on v3

--- a/solution.py
+++ b/solution.py
@@ -16,10 +16,10 @@
 LEAD = 2
 OWN = 6
 OWN_B = 3
-BEGUN = 5
+BEGUN = 6
 BEGUN_LOW = 6
-LAG = 5
-CUTS = 1
+LAG = 6
+CUTS = 2
 NEAR_LAG = 5
 
 
@@ -58,11 +58,9 @@
     sizes = []
     left = share
     while left:
-        size = min(size, left)
-        if left <= size:
-            size = max(1, left // 2)
-        sizes.append(size)
-        left -= size
+        now = size if 4 * left > share else max(1, size // 2)
+        sizes.append(min(now, left))
+        left -= sizes[-1]
     return sizes
 
 
@@ -70,7 +68,7 @@
     n, m, sizes, groups, block,
     field, tab_x, tab_y, tab_zh, tab_zl, sx, sy, sz, out,
     d, s, r, y, c, f, pass_on, tx, ty, tzh, tzl, colx, coly, vx, vy, vz,
-    in_sem, send_r, recv_r, send_c, recv_c, recv_p, up_r, up_c,
+    in_sem, send_r, recv_r, send_c, recv_c, recv_p, up_r, up_c, up_e,
 ):
     pieces = len(sizes)
     starts = [sum(sizes[:k]) for k in range(pieces)]
@@ -81,12 +79,15 @@
     cut = ys // CUTS
     fields = [pl.ds(i * cut, cut) for i in range(CUTS)]
     fields = [
-        pltpu.make_async_copy(field.at[:, at, :], d.at[:, at, :], in_sem.at[8 + i])
+        pltpu.make_async_copy(field.at[:, at, :], d.at[:, at, :], in_sem.at[2 + i])
         for i, at in enumerate(fields)
     ]
-    loads = [(tab_x, tx, 1), (tab_y, ty, 2), (tab_zh, tzh, 3), (tab_zl, tzl, 4)]
-    loads += [(sx, vx, 5), (sy, vy, 6), (sz, vz, 7)]
+    loads = [(tab_x, tx, 0), (tab_y, ty, 1), (tab_zh, tzh, 1), (tab_zl, tzl, 1)]
+    loads += [(sx, vx, 1), (sy, vy, 1), (sz, vz, 1)]
     loads = [pltpu.make_async_copy(a, b, in_sem.at[i]) for a, b, i in loads]
+
+    for load in fields + loads:
+        load.start()
 
     odd = lax.rem(me_r, 2)
     tier = lax.div(me_r, 2)
@@ -108,8 +109,6 @@
 
     lax.fori_loop(me_r + 1, n, greet_row, 0)
     lax.fori_loop(place(me_c) + 1, m, greet_col, 0)
-    for load in loads[:1] + fields + loads[1:]:
-        load.start()
     earlier = jnp.where(odd == 1, me_r, tier) + place(me_c)
 
     @pl.when(earlier > 0)
@@ -126,6 +125,11 @@
 
         lax.fori_loop(0, me_r, answer, 0)
 
+    @pl.when(me_r == 2 * (tiers // 2))
+    def _():
+        for at in range(tiers // 4, tiers // 2):
+            pl.semaphore_signal(up_e, inc=1, device_id={"row": 2 * at}, device_id_type=MESH)
+
     def answer_col(at, _):
         pl.semaphore_signal(up_c, inc=1, device_id={"col": place(at)}, device_id_type=MESH)
         return 0
@@ -136,7 +140,7 @@
     lanes = d.reshape(depth * ys, zs)
     modes = s.reshape(s.shape[0] * ys, zs)
 
-    def transform_x(first, count):
+    def transform_x(first, count, after=None):
         begin = n * starts[first]
         rows = n * sum(sizes[first : first + count])
         table = tx[2 * begin : 2 * (begin + rows)]
@@ -156,15 +160,18 @@
             if first == 0:
                 fields[i].wait()
             lax.fori_loop(i * cut // 2, (i + 1) * cut // 2, pair, 0, unroll=True)
+            if after is not None:
+                after(i)
 
     def rows_of(at):
         return pl.ds(pl.multiple_of(at * ys, ys), ys)
 
-    def send_row(k, to):
-        each = sizes[k]
+    def send_row(k, to, part=0, parts=1):
+        each, some = sizes[k], ys // parts
+        into = pl.ds(pl.multiple_of(me_r * ys + part * some, some), some)
         pltpu.make_async_remote_copy(
-            src_ref=s.at[pl.ds(n * starts[k] + to * each, each)],
-            dst_ref=r.at[pl.ds(starts[k], each), rows_of(me_r), :],
+            src_ref=s.at[pl.ds(n * starts[k] + to * each, each), pl.ds(part * some, some), :],
+            dst_ref=r.at[pl.ds(starts[k], each), into, :],
             send_sem=send_r,
             recv_sem=recv_r.at[k],
             device_id={"row": to},
@@ -245,16 +252,33 @@
         def _():
             wait_up(tier)
 
-    def start_far():
-        for other in range(2):
-            if other == 1:
-                hear_peer()
-
-            def one(at, _):
-                send_tier(0, at, other)
+    def start_far(part):
+        def same(at, _):
+            send_row(0, 2 * at + odd, part, CUTS)
+            return 0
+
+        lax.fori_loop(0, half, same, 0)
+
+        if part == CUTS - 1:
+            hear_peer()
+
+            def other(at, _):
+                send_tier(0, at, 1)
                 return 0
 
-            lax.fori_loop(0, half, one, 0)
+            lax.fori_loop(0, half, other, 0)
+
+    def start_low():
+        @pl.when(odd == 0)
+        def _():
+            pl.semaphore_wait(up_e, 1)
+            send_tier(0, half, 0)
+
+        @pl.when(odd == 1)
+        def _():
+            wait_up(half)
+            send_tier(0, half, 0)
+            send_tier(0, half, 1)
 
     def send_peer():
         for k in every:
@@ -283,19 +307,26 @@
         if 0 <= step - lead:
             part(step - lead, turn, end)
 
-    for at, (first, count) in enumerate(groups):
-        transform_x(first, count)
-        if at == 0:
-
-            @pl.when(jnp.logical_and(high, inner))
+    inner_high, inner_low = jnp.logical_and(high, inner), jnp.logical_and(low, inner)
+    begun_high, begun_low = min(BEGUN, pieces), min(BEGUN_LOW, pieces)
+
+    def first_sends(part):
+        @pl.when(inner_high)
+        def _():
+            start_far(part)
+
+        if part == CUTS - 1:
+
+            @pl.when(inner_low)
             def _():
-                start_far()
+                start_low()
 
             @pl.when(jnp.logical_and(high, outer))
             def _():
                 hand_on(0)
 
-    begun_high, begun_low = min(BEGUN, pieces), min(BEGUN_LOW, pieces)
+    for at, (first, count) in enumerate(groups):
+        transform_x(first, count, None if at else first_sends)
 
     @pl.when(jnp.logical_and(high, inner))
     def _():
@@ -303,12 +334,28 @@
         send_peer()
         send_tiers(every, tier + 1, tiers, wait=True)
 
-    @pl.when(jnp.logical_and(low, inner))
-    def _():
+    @pl.when(inner_low)
+    def _():
+        def more(own):
+            for k in range(1, own):
+                send_tier(k, half, 0)
+
+        by_core(more)
         hear_peer()
         send_tiers(every, 0, tier)
         send_peer()
-        for at in range(half, tiers):
+
+        @pl.when(odd == 0)
+        def _():
+            wait_up(half)
+            send_tier(0, half, 1)
+
+        def others(own):
+            for k in range(1, own):
+                send_tier(k, half, 1)
+
+        by_core(others)
+        for at in range(half + 1, tiers):
             wait_up(at)
             by_core(lambda own: send_tiers(range(own), at, at + 1))
 
@@ -347,8 +394,6 @@
         return [at for at in range(step, pieces + lead) if at == step or step == pieces - 1] * (
             step < pieces
         )
-
-    inner_high, inner_low = jnp.logical_and(high, inner), jnp.logical_and(low, inner)
 
     @pl.when(inner_high)
     def _():
@@ -413,11 +458,12 @@
 
         def one(i, _):
             to = lax.rem(me_c + i, m)
+            beside = (lax.div(to, m // 2) == side).astype(jnp.int32) if k == pieces - 1 else 0
             pltpu.make_async_remote_copy(
                 src_ref=y.at[pl.ds(base + to * each, each)],
                 dst_ref=c.at[pl.ds(base + me_c * each, each)],
                 send_sem=send_c,
-                recv_sem=recv_c.at[k],
+                recv_sem=recv_c.at[k + beside],
                 device_id={"col": to},
                 device_id_type=MESH,
             ).start()
@@ -430,6 +476,26 @@
     def got_cols(k):
         waited = c.at[pl.ds(m * starts[k], (m - 1) * sizes[k])]
         pltpu.make_async_copy(waited, waited, recv_c.at[k]).wait()
+
+    side = lax.div(me_c, m // 2)
+
+    def half_z(at_side, count, sem):
+        k = pieces - 1
+        each, base = sizes[k], m * starts[k]
+        rows, many = each * yc, m // 2 * zs
+        if count:
+            waited = c.at[pl.ds(base, count * each)]
+            pltpu.make_async_copy(waited, waited, recv_c.at[sem]).wait()
+        got = [
+            c[pl.ds(base + (at_side * (m // 2) + q) * each, each)].reshape(rows, zs)
+            for q in range(m // 2)
+        ]
+        high, low = halves(jnp.concatenate(got, axis=1))
+        some = pl.ds(pl.multiple_of(at_side * many, many), many)
+        both = dot(jnp.concatenate([high, low], axis=0), tzh[some, :])
+        return both[:rows] + both[rows:] + dot(high, tzl[some, :])
+
+    last_rows = slice(starts[pieces - 1] * yc, (starts[pieces - 1] + sizes[pieces - 1]) * yc)
 
     def transform_z(k):
         each, base = sizes[k], m * starts[k]
@@ -473,7 +539,11 @@
 
     for k in range(pieces - lag, pieces):
         if k == pieces - 1:
+            out[last_rows, :] = (out[last_rows, :] + half_z(1 - side, m // 2, k)) * f[last_rows, :]
+            break
+        if k == max(pieces - 2, pieces - lag):
             sent_all()
+            out[last_rows, :] = half_z(side, m // 2 - 1, pieces)
 
             @pl.when(jnp.logical_and(low, outer))
             def _():
@@ -539,13 +609,14 @@
             pltpu.VMEM((1, depth), F32),
             pltpu.VMEM((1, height), F32),
             pltpu.VMEM((1, length), F32),
-            dma((8 + CUTS,)),
+            dma((2 + CUTS,)),
             dma,
             dma((pieces,)),
             dma,
-            dma((pieces,)),
+            dma((pieces + 1,)),
             dma((pieces,)),
             regular((n // 2,)),
+            regular,
             regular,
         ],
         compiler_params=pltpu.CompilerParams(

time: 32.9 us -> 32.4 us (0.985); the launches traced: 32.4 us -> 32.3 us
  no operation moved by 1% of the time
where the time goes in v4:
time: 32.4 us; the launch traced here: 32.3 us
  Pallas kernels  31.3 us (97%)
  local copies, waits for them, and re-layouts  0.97 us (3%)
    pallas_call x1, Pallas kernels, per_device(): pl.pallas_call(functools.partial(kernel, n, m, sizes, groups, block), out...  31.3 us
    unnamed x1, local copies, waits for them, and re-layouts  0.97 us

profile of v4, /device:TPU:0, one launch (start us, length us, event | category | flops | bytes accessed | tf_op | source)
XLA Modules:
  0.0 32.3 jit_solution(8957818154577855463)
XLA Ops:
  0.0 31.3 %shard_map.82 = f32[512,512]{1,0:T(8,128)S(1)} custom-call(f32[128,16,128]{2,1,0:T(8,128)} %field.1, bf16[256,256]{1,0:T(8,128)(2,1)} %constant.8.clone.tab_x, bf16[256,256]{1,0:T(8,128)(2,1)} %constant.9.clone.tab_y, bf16[512,512]{1,0:T(8,128)(2,1)} %constant.10.clone.tab_zh, bf16[512,512]{1,0:T(8,128)(2,1)} %constant.11.clone.tab_zl, f32[1,128]{1,0:T(1,128)} %bitcast.6, ...), custom_call_target="tpu_custom_call" | custom-call | tf_op jit(solution)/shard_map/pallas_call | solution.py:590
  31.3 1.0 %copy.10 = f32[16,32,512]{2,1,0:T(8,128)} copy(f32[16,32,512]{2,1,0:T(8,128)S(1)} %bitcast.4) | data formatting | bytes 2097152

commit v5 on v4

--- a/solution.py
+++ b/solution.py
@@ -13,11 +13,11 @@
 F32 = jnp.float32
 BF16 = jnp.bfloat16
 PIECES = 8
-LEAD = 2
-OWN = 6
+LEAD = 3
+OWN = 7
 OWN_B = 3
 BEGUN = 6
-BEGUN_LOW = 6
+BEGUN_LOW = 7
 LAG = 6
 CUTS = 2
 NEAR_LAG = 5

time: 32.4 us -> 32.4 us (level)
  no operation moved by 1% of the time
where the time goes in v5:
time: 32.4 us; the launch traced here: 32.1 us
  Pallas kernels  31.1 us (96%)
  local copies, waits for them, and re-layouts  0.97 us (3%)
    pallas_call x1, Pallas kernels, per_device(): pl.pallas_call(functools.partial(kernel, n, m, sizes, groups, block), out...  31.1 us
    unnamed x1, local copies, waits for them, and re-layouts  0.97 us

profile of v5, /device:TPU:0, one launch (start us, length us, event | category | flops | bytes accessed | tf_op | source)
XLA Modules:
  0.0 32.1 jit_solution(2965431416620731492)
XLA Ops:
  0.0 31.1 %shard_map.82 = f32[512,512]{1,0:T(8,128)S(1)} custom-call(f32[128,16,128]{2,1,0:T(8,128)} %field.1, bf16[256,256]{1,0:T(8,128)(2,1)} %constant.8.clone.tab_x, bf16[256,256]{1,0:T(8,128)(2,1)} %constant.9.clone.tab_y, bf16[512,512]{1,0:T(8,128)(2,1)} %constant.10.clone.tab_zh, bf16[512,512]{1,0:T(8,128)(2,1)} %constant.11.clone.tab_zl, f32[1,128]{1,0:T(1,128)} %bitcast.6, ...), custom_call_target="tpu_custom_call" | custom-call | tf_op jit(solution)/shard_map/pallas_call | solution.py:590
  31.1 1.0 %copy.10 = f32[16,32,512]{2,1,0:T(8,128)} copy(f32[16,32,512]{2,1,0:T(8,128)S(1)} %bitcast.4) | data formatting | bytes 2097152
